TPU v7x, 256 devices: a whole 4x4x8 slice. The times are simulated.
256 devices in a mesh: wide: 64 (over y, z_lo, x), layer: 4 (over z_hi, core).
Axes of the slice: x: 4, y: 4, z: 8 (z_hi: 2, z_lo: 4; z = z_hi * 4 + z_lo), core: 2. Of those that a mesh axis runs over, the one named last changes fastest.
Arguments:
- factor: float32 [32768, 8192], P('layer', 'wide'), parts along dimension 0, may hold values from -1 to 21, as said below
Outputs:
- rotated: float32 [32768, 8192], P('layer', 'wide'), parts along dimension 0
- eigen_basis: float32 [32768, 8192], P('layer', 'wide'), parts along dimension 0
There are 4 independent parts, one for each index of `layer`. A program takes and returns all parts, laid end to end along the dimension named above; each array names one. Nothing has to cross between parts.
Inputs may be any that keep to these rules, and one draw needn't show every extreme that they name: `factor`: symmetric.
All inputs are finite; a program needn't handle non-finite values.
Results may differ from a plain program's by a relative error of at most 0.00095.
Values sent between devices are 32-bit elements; how exact they have to be, the bound alone decides.
A program may use at most 128 MiB of HBM per device.

v0:
```python
import jax
import jax.numpy as jnp
from jax import lax
from jax.sharding import Mesh
from jax.sharding import PartitionSpec as P

SWEEPS = 3
WIDE = ("wide_0", "wide_1", "wide_2")
floor_term = 0.01


def laid_out(parts, dim):
    dims = list(parts.shape[1:])
    dims[dim] *= parts.shape[0]
    return jnp.moveaxis(parts, 0, dim).reshape(dims)


def gather_in_order(shard, axes, order):
    parts = shard[None]
    for k in order:
        parts = lax.all_gather(parts, axes[k], axis=0, tiled=True)
    held = [lax.axis_size(axes[k]) for k in reversed(order)]
    parts = parts.reshape(*held, *shard.shape)
    turned = sorted(range(len(order)), key=lambda place: order[len(order) - 1 - place])
    return parts.transpose(*turned, *range(len(order), parts.ndim)).reshape(-1, *shard.shape)


def whole_of(shard, axes, order, dim):
    return laid_out(gather_in_order(shard, axes, order), dim)


def from_partner(shard, axis, bit):
    return lax.ppermute(shard, axis, [(i, i ^ 1 << bit) for i in range(lax.axis_size(axis))])


def cayley_sweeps(pair_block):
    order_size = pair_block.shape[0]
    identity_mat = jnp.eye(order_size, dtype=pair_block.dtype)
    rotation = identity_mat
    for repeat in range(SWEEPS):
        diagonal = jnp.diagonal(pair_block)
        spread = diagonal[None, :] - diagonal[:, None]
        ratios = (
            pair_block * spread / (spread * spread + 2.0 * pair_block * pair_block + floor_term)
        )
        skewed = 0.5 * (ratios - ratios.T) * (1.0 - identity_mat)
        half_turn = identity_mat + 0.5 * skewed
        system = identity_mat - 0.25 * jnp.dot(skewed, skewed, precision=lax.Precision.HIGHEST)
        lower_part = jnp.linalg.cholesky(system)
        square_turn = jnp.dot(half_turn, half_turn, precision=lax.Precision.HIGHEST)
        rotate_now = jax.scipy.linalg.cho_solve((lower_part, True), square_turn)
        pair_block = jnp.dot(
            rotate_now.T,
            jnp.dot(pair_block, rotate_now, precision=lax.Precision.HIGHEST),
            precision=lax.Precision.HIGHEST,
        )
        rotation = jnp.dot(rotation, rotate_now, precision=lax.Precision.HIGHEST)
    return rotation


def trade_rows(current, wide_count, width_half):
    order_size, pair_span = current.shape
    split_view = current.reshape(2, wide_count // 2, 2, width_half, pair_span)
    joined = jnp.concatenate([split_view[:, :, :1], split_view[::-1, :, 1:]], axis=2)
    return joined.reshape(order_size, pair_span)


def one_round(current, basis, my_pair):
    order_size, pair_span = current.shape
    pair_block = lax.dynamic_slice_in_dim(current, my_pair * pair_span, pair_span, 0)
    rotate = cayley_sweeps(pair_block)
    columns = jnp.dot(current, rotate, precision=lax.Precision.HIGHEST)
    pieces = whole_of(rotate[None], WIDE, (1, 0, 2), 0)
    how_many = pieces.shape[0]
    row_slab = columns
    row_slab = row_slab.reshape(how_many, pair_span, pair_span)
    updated = jnp.einsum("nba,nbc->nac", pieces, row_slab, precision=lax.Precision.HIGHEST)
    current = lax.dynamic_update_slice_in_dim(
        columns, updated.reshape(how_many * pair_span, pair_span), jnp.int32(0) * pair_span, 0
    )
    basis = jnp.dot(basis, rotate, precision=lax.Precision.HIGHEST)
    return (current, basis)


def body(factor):
    wide_count = lax.axis_size(WIDE)
    my_pair = lax.axis_index(WIDE)
    order_size, pair_span = factor.shape
    width_half = pair_span // 2
    row_index = lax.broadcasted_iota(jnp.int32, (order_size, pair_span), 0)
    col_index = lax.broadcasted_iota(jnp.int32, (order_size, pair_span), 1) + my_pair * pair_span
    basis = (row_index == col_index).astype(jnp.float32)
    current = factor
    for repeat in range(2):
        if repeat == 1:
            moved_factor, moved_basis = from_partner(
                (current[:, width_half:], basis[:, width_half:]), WIDE, wide_count.bit_length() - 2
            )
            current = jnp.concatenate([current[:, :width_half], moved_factor], axis=1)
            basis = jnp.concatenate([basis[:, :width_half], moved_basis], axis=1)
            current = trade_rows(current, wide_count, width_half)
        current, basis = one_round(current, basis, my_pair)
    return (current, basis)


def solution(mesh):
    finer = Mesh(
        mesh.devices.reshape(4, 4, 4, mesh.shape["layer"]), ("wide_0", "wide_1", "wide_2", "layer")
    )
    in_specs = (P("layer", WIDE),)
    out_specs = (P("layer", WIDE), P("layer", WIDE))
    return jax.shard_map(body, mesh=finer, in_specs=in_specs, out_specs=out_specs, check_vma=False)
```

profile of v0, /device:TPU:2, one launch (start us, length us, event | category | flops | bytes accessed | tf_op | source)
XLA Modules:
  0.0 474.6 jit_solution(8822284381728006457)
XLA Ops:
  7.2 0.8 constant_dynamic-slice_fusion.1
  8.2 1.3 gather_fusion
  10.3 11.7 %cholesky.104 = f32[128,128]{1,0:T(8,128)S(1)} custom-call(f32[128,128]{1,0:T(8,128)S(1)} %fusion.100), custom_call_target="Cholesky" | custom-call | tf_op jit(solution)/shard_map/jit(cholesky)/cholesky | solution.py:49
  22.7 0.7 fusion.18
  23.4 9.8 %custom-call.24 = f32[1,128,128]{1,2,0:T(8,128)S(1)} custom-call(f32[1,128,128]{2,1,0:T(8,128)S(1)} %fusion.18), custom_call_target="InvertDiagBlocksLowerTriangular" | custom-call | tf_op jit(solution)/shard_map/jit(_cho_solve)/triangular_solve | solution.py:51
  34.5 1.7 gather_fusion.1
  37.0 11.7 %cholesky.115 = f32[128,128]{1,0:T(8,128)S(1)} custom-call(f32[128,128]{1,0:T(8,128)S(1)} %fusion.95), custom_call_target="Cholesky" | custom-call | tf_op jit(solution)/shard_map/jit(cholesky)/cholesky | solution.py:49
  49.4 0.7 fusion.19
  50.1 9.8 %custom-call.25 = f32[1,128,128]{1,2,0:T(8,128)S(1)} custom-call(f32[1,128,128]{2,1,0:T(8,128)S(1)} %fusion.19), custom_call_target="InvertDiagBlocksLowerTriangular" | custom-call | tf_op jit(solution)/shard_map/jit(_cho_solve)/triangular_solve | solution.py:51
  61.0 1.4 gather_fusion.2
  63.4 11.7 %cholesky.126 = f32[128,128]{1,0:T(8,128)S(1)} custom-call(f32[128,128]{1,0:T(8,128)S(1)} %fusion.90), custom_call_target="Cholesky" | custom-call | tf_op jit(solution)/shard_map/jit(cholesky)/cholesky | solution.py:49
  75.8 0.7 fusion.20
  76.4 9.8 %custom-call.26 = f32[1,128,128]{1,2,0:T(8,128)S(1)} custom-call(f32[1,128,128]{2,1,0:T(8,128)S(1)} %fusion.20), custom_call_target="InvertDiagBlocksLowerTriangular" | custom-call | tf_op jit(solution)/shard_map/jit(_cho_solve)/triangular_solve | solution.py:51
  86.9 15.6 %all-gather = f32[512,128]{1,0:T(8,128)} all-gather(f32[128,128]{1,0:T(8,128)S(1)} %fusion.147), channel_id=2, replica_groups=mesh['wide_0'=4,'wide_1'=4,'wide_2'=4,'layer'=4] {'wide_1'}, dimensions={0}, use_global_device_ids=true | all-gather | bytes 327680 | tf_op jit(solution)/shard_map/all_gather | solution.py:21
  102.6 28.8 %all-gather.7.cloned.1.call-done = f32[16,1,128,128]{3,2,1,0:T(8,128)} async-done(((f32[4,1,128,128]{3,2,1,0:T(8,128)}), f32[16,1,128,128]{3,2,1,0:T(8,128)}) %all-gather.7.cloned.1.call-update) | async-done | bytes 1048592 | tf_op jit(solution)/shard_map/all_gather | solution.py:21
  131.4 8.1 %convolution_bitcast_fusion = f32[8192,128]{0,1:T(8,128)} fusion(f32[128,128]{1,0:T(8,128)S(1)} %fusion.147, f32[8192,128]{1,0:T(8,128)} %param.4), kind=kOutput, calls=%fused_computation.6 | convolution fusion | flops 1610612736 | bytes 8454144 | tf_op jit(solution)/shard_map/dot_general | solution.py:72
  139.5 5.8 %copy.106 = f32[8192,128]{1,0:T(8,128)} copy(f32[8192,128]{0,1:T(8,128)} %convolution_bitcast_fusion) | data formatting | bytes 8388608 | tf_op jit(solution)/shard_map/reshape | solution.py:76
  145.3 38.4 %all-gather.9.cloned.1.call-done = f32[64,1,128,128]{3,2,1,0:T(8,128)} async-done(((f32[16,1,128,128]{3,2,1,0:T(8,128)}), f32[64,1,128,128]{3,2,1,0:T(8,128)}) %all-gather.9.cloned.1.call-update) | async-done | bytes 4194320 | tf_op jit(solution)/shard_map/all_gather | solution.py:21
  183.7 5.2 %copy.80 = f32[4,4,4,1,128,128]{4,5,0,2,1,3:T(8,128)} copy(f32[4,4,4,1,128,128]{5,4,2,1,0,3:T(8,128)} %bitcast.185) | data formatting | bytes 8388608 | tf_op jit(solution)/shard_map/reshape | solution.py:23
  188.9 6.6 %fusion.148 = f32[64,128,128]{2,1,0:T(8,128)S(1)} fusion(f32[64,128,128]{1,2,0:T(8,128)} %bitcast.181, f32[64,128,128]{2,1,0:T(8,128)} %bitcast.179), kind=kOutput, calls=%fused_computation.227 | convolution fusion | flops 1610612736 | bytes 12582912 | tf_op jit(solution)/shard_map/nba,nbc->nac/dot_general | solution.py:77
  195.5 4.7 fusion.141
  200.2 2.8 copy.82
  203.1 3.1 collective-permute-start
  206.2 45.8 %collective-permute-done = f32[8192,64]{0,1:T(8,128)} collective-permute-done((f32[8192,64]{0,1:T(8,128)S(1)}, f32[8192,64]{0,1:T(8,128)}, u32[]{:S(2)}, u32[]{:S(2)}) %collective-permute-start) | collective-permute-done | bytes 2097184 | tf_op jit(solution)/shard_map/ppermute | solution.py:33
  252.0 3.8 copy.83
  255.8 4.6 pad_maximum_fusion
  260.4 1.7 fusion.140
  262.1 1.5 rev.3
  263.6 2.5 pad_maximum_fusion.1
  266.1 2.0 copy-done
  268.2 1.3 gather_fusion.3
  270.4 11.7 %cholesky.137 = f32[128,128]{1,0:T(8,128)S(1)} custom-call(f32[128,128]{1,0:T(8,128)S(1)} %fusion.84), custom_call_target="Cholesky" | custom-call | tf_op jit(solution)/shard_map/jit(cholesky)/cholesky | solution.py:49
  283.4 9.8 %custom-call.27 = f32[1,128,128]{1,2,0:T(8,128)S(1)} custom-call(f32[1,128,128]{2,1,0:T(8,128)S(1)} %fusion.21), custom_call_target="InvertDiagBlocksLowerTriangular" | custom-call | tf_op jit(solution)/shard_map/jit(_cho_solve)/triangular_solve | solution.py:51
  294.6 1.7 gather_fusion.4
  297.0 11.7 %cholesky.148 = f32[128,128]{1,0:T(8,128)S(1)} custom-call(f32[128,128]{1,0:T(8,128)S(1)} %fusion.79), custom_call_target="Cholesky" | custom-call | tf_op jit(solution)/shard_map/jit(cholesky)/cholesky | solution.py:49
  310.1 9.8 %custom-call.28 = f32[1,128,128]{1,2,0:T(8,128)S(1)} custom-call(f32[1,128,128]{2,1,0:T(8,128)S(1)} %fusion.22), custom_call_target="InvertDiagBlocksLowerTriangular" | custom-call | tf_op jit(solution)/shard_map/jit(_cho_solve)/triangular_solve | solution.py:51
  321.0 1.4 gather_fusion.5
  323.4 11.7 %cholesky.159 = f32[128,128]{1,0:T(8,128)S(1)} custom-call(f32[128,128]{1,0:T(8,128)S(1)} %fusion.74), custom_call_target="Cholesky" | custom-call | tf_op jit(solution)/shard_map/jit(cholesky)/cholesky | solution.py:49
  336.4 9.8 %custom-call.29 = f32[1,128,128]{1,2,0:T(8,128)S(1)} custom-call(f32[1,128,128]{2,1,0:T(8,128)S(1)} %fusion.23), custom_call_target="InvertDiagBlocksLowerTriangular" | custom-call | tf_op jit(solution)/shard_map/jit(_cho_solve)/triangular_solve | solution.py:51
  346.9 14.8 %all-gather.1 = f32[512,128]{1,0:T(8,128)} all-gather(f32[128,128]{1,0:T(8,128)S(1)} %fusion.154), channel_id=3, replica_groups=mesh['wide_0'=4,'wide_1'=4,'wide_2'=4,'layer'=4] {'wide_1'}, dimensions={0}, use_global_device_ids=true | all-gather | bytes 327680 | tf_op jit(solution)/shard_map/all_gather | solution.py:21
  361.8 28.0 %all-gather.11.cloned.1.call-done = f32[16,1,128,128]{3,2,1,0:T(8,128)} async-done(((f32[4,1,128,128]{3,2,1,0:T(8,128)}), f32[16,1,128,128]{3,2,1,0:T(8,128)}) %all-gather.11.cloned.1.call-update) | async-done | bytes 1048592 | tf_op jit(solution)/shard_map/all_gather | solution.py:21
  389.9 2.1 fusion.4
  392.4 2.2 collective-permute-start.1
  394.6 44.7 %collective-permute-done.1 = f32[8192,64]{0,1:T(8,128)S(1)} collective-permute-done((f32[8192,64]{0,1:T(8,128)S(1)}, f32[8192,64]{0,1:T(8,128)S(1)}, u32[]{:S(2)}, u32[]{:S(2)}) %collective-permute-start.1) | collective-permute-done | bytes 2097184 | tf_op jit(solution)/shard_map/ppermute | solution.py:33
  439.3 8.5 %fusion = f32[8192,128]{1,0:T(8,128)} fusion(f32[128,128]{1,0:T(8,128)S(1)} %fusion.154, f32[8192,64]{0,1:T(8,128)S(1)} %collective-permute-done.1, f32[8192,64]{0,1:T(8,128)S(1)} %get-tuple-element.4), kind=kOutput, calls=%fused_computation.9 | convolution fusion | flops 1611661312 | bytes 8454144 | tf_op jit(solution)/shard_map/dot_general | solution.py:81
  447.8 4.9 %fusion.68 = f32[64,128,128]{2,1,0:T(8,128)} fusion(f32[64,128,128]{2,1,0:T(8,128)S(1)} %bitcast.178, f32[128,128]{1,0:T(8,128)S(1)} %fusion.154), kind=kOutput, calls=%fused_computation.127 | convolution fusion | flops 1610612736 | bytes 8454144 | tf_op jit(solution)/shard_map/dot_general | solution.py:72
  452.7 5.2 %copy.99 = f32[4,4,4,1,128,128]{4,5,0,2,1,3:T(8,128)} copy(f32[4,4,4,1,128,128]{5,4,2,1,0,3:T(8,128)} %bitcast.184) | data formatting | bytes 8388608 | tf_op jit(solution)/shard_map/reshape | solution.py:23
  458.0 9.9 %fusion.155 = f32[64,128,128]{2,1,0:T(8,128)} fusion(f32[64,128,128]{1,2,0:T(8,128)} %bitcast.182, f32[64,128,128]{2,1,0:T(8,128)} %fusion.68), kind=kOutput, calls=%fused_computation.234 | convolution fusion | flops 1610612736 | bytes 12582912 | tf_op jit(solution)/shard_map/nba,nbc->nac/dot_general | solution.py:77
  (95 shorter events, 17.8 us)
Async XLA Ops:
  7.2 124.2 %all-gather.7.cloned.1.call-start = ((), (), s32[]{:S(2)}) async-start(), calls=%async_computation | async-start | bytes 1310720 | tf_op jit(solution)/shard_map/all_gather | solution.py:21
  102.5 81.1 %all-gather.9.cloned.1.call-start = ((), (), s32[]{:S(2)}) async-start(), calls=%async_computation.1 | async-start | bytes 5242880 | tf_op jit(solution)/shard_map/all_gather | solution.py:21
  131.4 258.5 %all-gather.11.cloned.1.call-start = ((), (), s32[]{:S(2)}) async-start(), calls=%async_computation.2 | async-start | bytes 1310720 | tf_op jit(solution)/shard_map/all_gather | solution.py:21
  203.1 48.9 %collective-permute-start = (f32[8192,64]{0,1:T(8,128)S(1)}, f32[8192,64]{0,1:T(8,128)}, u32[]{:S(2)}, u32[]{:S(2)}) collective-permute-start(f32[8192,64]{0,1:T(8,128)S(1)} %copy.82), channel_id=1, source_target_pairs={{0,128},{4,132},{8,136},{12,140},{16,144},{20,148},{24,152},{28,15... | collective-permute-start | bytes 6291464 | tf_op jit(solution)/shard_map/ppermute | solution.py:33
  266.1 2.0 copy-start
  361.8 90.9 %all-gather.13.cloned.1.call-start = ((), (), s32[]{:S(2)}) async-start(), calls=%async_computation.3 | async-start | bytes 5242880 | tf_op jit(solution)/shard_map/all_gather | solution.py:21
  392.4 46.9 %collective-permute-start.1 = (f32[8192,64]{0,1:T(8,128)S(1)}, f32[8192,64]{0,1:T(8,128)S(1)}, u32[]{:S(2)}, u32[]{:S(2)}) collective-permute-start(f32[8192,64]{0,1:T(8,128)S(1)} %get-tuple-element.5), channel_id=1, source_target_pairs={{0,128},{4,132},{8,136},{12,140},{16,144},{20,148},{24,152},{28,15... | collective-permute-start | bytes 6291464 | tf_op jit(solution)/shard_map/ppermute | solution.py:33
  439.3 8.5 %copy-start.1 = (f32[2,32,2,64,128]{4,3,2,1,0:T(8,128)S(1)}, f32[2,32,2,64,128]{4,3,2,1,0:T(8,128)}, u32[]{:S(2)}) copy-start(f32[2,32,2,64,128]{4,3,2,1,0:T(8,128)} %copy-done) | copy-start | bytes 12582916
Sparse Core Ops, SparseCore 0:
  102.6 28.6 all-gather.6
  133.2 50.4 all-gather.8
  361.9 27.9 all-gather.10
  391.5 50.4 all-gather.12
where the time goes:
time: 481 us; the launch traced here: 475 us
  waiting for transfers between devices  186 us (39%)
  other arithmetic  145 us (30%)
  matrix products  49.3 us (10%)
  local copies, waits for them, and re-layouts  44 us (9%)
  blocking collectives  30.4 us (6%)
  between operations  14.7 us (3%)
  starting transfers between devices  5.42 us (1%)
    all_gather x4, waiting for transfers between devices, gather_in_order(): parts = lax.all_gather(parts, axes[k], axis=0, tiled=True)  95.2 us
    ppermute x2, waiting for transfers between devices, from_partner(): lax.ppermute(shard, axis, [(i, i ^ 1 << bit) for i in range(lax.axis_size...  90.5 us
    another operation x18, other arithmetic, cayley_sweeps(): lower_part = jnp.linalg.cholesky(system)  74.3 us
    another operation x12, other arithmetic, cayley_sweeps(): rotate_now = jax.scipy.linalg.cho_solve((lower_part, True), square_turn)  62.8 us
    all_gather x2, blocking collectives, gather_in_order(): parts = lax.all_gather(parts, axes[k], axis=0, tiled=True)  30.4 us
    dot_general x2, matrix products, one_round(): jnp.einsum('nba,nbc->nac', pieces, row_slab, precision=lax.Precision.HIGH...  16.5 us
    dot_general x2, matrix products, one_round(): columns = jnp.dot(current, rotate, precision=lax.Precision.HIGHEST)  13 us
    dot_general x2, matrix products, one_round(): basis = jnp.dot(basis, rotate, precision=lax.Precision.HIGHEST)  10.6 us
  transfers between devices with their start and end apart: 6, of which 5 were waited for; matrix products, arithmetic and copies ran while one was open for 6% of the time, Pallas kernels for 0%

commit v1 on v0

--- a/solution.py
+++ b/solution.py
@@ -18,7 +18,9 @@
 def gather_in_order(shard, axes, order):
     parts = shard[None]
     for k in order:
-        parts = lax.all_gather(parts, axes[k], axis=0, tiled=True)
+        parts = jnp.concatenate(
+            lax.all_to_all(jnp.stack([parts] * lax.axis_size(axes[k])), axes[k], 0, 0), axis=0
+        )
     held = [lax.axis_size(axes[k]) for k in reversed(order)]
     parts = parts.reshape(*held, *shard.shape)
     turned = sorted(range(len(order)), key=lambda place: order[len(order) - 1 - place])

time: 481 us -> 434 us (0.902)
  waiting for transfers between devices: 186 us -> 123 us
  blocking collectives: 30.4 us -> 46.4 us
  between operations: 14.7 us -> 1.61 us
  starting transfers between devices: 5.42 us -> 16.5 us
  local copies, waits for them, and re-layouts: 44 us -> 49.2 us
    all_gather x4 -> x0, waiting for transfers between devices: 95.2 us -> none  [gather_in_order(): parts = lax.all_gather(parts, axes[k], axis=0, tiled=True)]
    all_to_all x0 -> x3, blocking collectives: none -> 46.4 us  [gather_in_order(): lax.all_to_all(jnp.stack([parts] * lax.axis_size(axes[k])), axes[k], 0, 0)]
    all_to_all x0 -> x3, waiting for transfers between devices: none -> 37.3 us  [gather_in_order(): lax.all_to_all(jnp.stack([parts] * lax.axis_size(axes[k])), axes[k], 0, 0)]
    all_gather x2 -> x0, blocking collectives: 30.4 us -> none  [gather_in_order(): parts = lax.all_gather(parts, axes[k], axis=0, tiled=True)]
    all_to_all x0 -> x3, starting transfers between devices: none -> 15.3 us  [gather_in_order(): lax.all_to_all(jnp.stack([parts] * lax.axis_size(axes[k])), axes[k], 0, 0)]
    another operation x0 -> x8, local copies, waits for them, and re-layouts: none -> 11.5 us  [the longest x6 6.33 us: gather_in_order(): jnp.stack([parts] * lax.axis_size(axes[k]))]
    reshape x2 -> x0, local copies, waits for them, and re-layouts: 10.5 us -> none  [gather_in_order(): parts = parts.reshape(*held, *shard.shape)]
    dot_general x2, matrix products: 16.5 us -> 10.6 us  [one_round(): jnp.einsum('nba,nbc->nac', pieces, row_slab, precision=lax.Precision.HIGH...]
  transfers between devices with their start and end apart: 6 -> 5, of which waited for: 5 -> 4; matrix products, arithmetic and copies ran while one was open for 6% -> 8% of each run, Pallas kernels for 0% -> 0%
where the time goes in v1:
time: 434 us; the launch traced here: 427 us
  other arithmetic  145 us (33%)
  waiting for transfers between devices  123 us (28%)
  local copies, waits for them, and re-layouts  49.2 us (11%)
  blocking collectives  46.4 us (11%)
  matrix products  45.5 us (10%)
  starting transfers between devices  16.5 us (4%)
    ppermute x2, waiting for transfers between devices, from_partner(): lax.ppermute(shard, axis, [(i, i ^ 1 << bit) for i in range(lax.axis_size...  86.1 us
    another operation x18, other arithmetic, cayley_sweeps(): lower_part = jnp.linalg.cholesky(system)  74.3 us
    another operation x12, other arithmetic, cayley_sweeps(): rotate_now = jax.scipy.linalg.cho_solve((lower_part, True), square_turn)  62.8 us
    all_to_all x3, blocking collectives, gather_in_order(): lax.all_to_all(jnp.stack([parts] * lax.axis_size(axes[k])), axes[k], 0, 0)  46.4 us
    all_to_all x3, waiting for transfers between devices, gather_in_order(): lax.all_to_all(jnp.stack([parts] * lax.axis_size(axes[k])), axes[k], 0, 0)  37.3 us
    all_to_all x3, starting transfers between devices, gather_in_order(): lax.all_to_all(jnp.stack([parts] * lax.axis_size(axes[k])), axes[k], 0, 0)  15.3 us
    dot_general x2, matrix products, one_round(): columns = jnp.dot(current, rotate, precision=lax.Precision.HIGHEST)  13 us
    dot_general x2, matrix products, one_round(): basis = jnp.dot(basis, rotate, precision=lax.Precision.HIGHEST)  12.7 us
  transfers between devices with their start and end apart: 5, of which 4 were waited for; matrix products, arithmetic and copies ran while one was open for 8% of the time, Pallas kernels for 0%

profile of v1, /device:TPU:2, one launch (start us, length us, event | category | flops | bytes accessed | tf_op | source)
XLA Modules:
  0.0 427.5 jit_solution(3535773446599772634)
XLA Ops:
  1.6 1.3 gather_fusion
  3.7 11.7 %cholesky.104 = f32[128,128]{1,0:T(8,128)S(1)} custom-call(f32[128,128]{1,0:T(8,128)S(1)} %fusion.100), custom_call_target="Cholesky" | custom-call | tf_op jit(solution)/shard_map/jit(cholesky)/cholesky | solution.py:51
  16.8 9.8 %custom-call.24 = f32[1,128,128]{1,2,0:T(8,128)S(1)} custom-call(f32[1,128,128]{2,1,0:T(8,128)S(1)} %fusion.18), custom_call_target="InvertDiagBlocksLowerTriangular" | custom-call | tf_op jit(solution)/shard_map/jit(_cho_solve)/triangular_solve | solution.py:53
  28.0 1.5 gather_fusion.1
  30.3 11.7 %cholesky.115 = f32[128,128]{1,0:T(8,128)S(1)} custom-call(f32[128,128]{1,0:T(8,128)S(1)} %fusion.95), custom_call_target="Cholesky" | custom-call | tf_op jit(solution)/shard_map/jit(cholesky)/cholesky | solution.py:51
  43.3 9.8 %custom-call.25 = f32[1,128,128]{1,2,0:T(8,128)S(1)} custom-call(f32[1,128,128]{2,1,0:T(8,128)S(1)} %fusion.19), custom_call_target="InvertDiagBlocksLowerTriangular" | custom-call | tf_op jit(solution)/shard_map/jit(_cho_solve)/triangular_solve | solution.py:53
  54.2 1.8 gather_fusion.2
  57.0 11.7 %cholesky.126 = f32[128,128]{1,0:T(8,128)S(1)} custom-call(f32[128,128]{1,0:T(8,128)S(1)} %fusion.90), custom_call_target="Cholesky" | custom-call | tf_op jit(solution)/shard_map/jit(cholesky)/cholesky | solution.py:51
  70.0 9.8 %custom-call.26 = f32[1,128,128]{1,2,0:T(8,128)S(1)} custom-call(f32[1,128,128]{2,1,0:T(8,128)S(1)} %fusion.20), custom_call_target="InvertDiagBlocksLowerTriangular" | custom-call | tf_op jit(solution)/shard_map/jit(_cho_solve)/triangular_solve | solution.py:53
  80.7 14.6 %all_to_all.30 = f32[4,1,1,128,128]{3,4,2,1,0:T(8,128)S(1)} all-to-all(f32[4,1,1,128,128]{3,4,2,1,0:T(8,128)S(1)} %stack.18), channel_id=1, replica_groups=mesh['wide_0'=4,'wide_1'=4,'wide_2'=4,'layer'=4] {'wide_1'}, dimensions={0} | all-to-all | bytes 524288 | tf_op jit(solution)/shard_map/all_to_all | solution.py:22
  95.3 17.0 %all_to_all.31 = f32[4,4,1,128,128]{3,4,1,2,0:T(8,128)S(1)} all-to-all(f32[4,4,1,128,128]{3,4,1,2,0:T(8,128)S(1)} %stack.19), channel_id=1, replica_groups=mesh['wide_0'=4,'wide_1'=4,'wide_2'=4,'layer'=4] {'wide_0'}, dimensions={0} | all-to-all | bytes 2097152 | tf_op jit(solution)/shard_map/all_to_all | solution.py:22
  112.4 2.5 stack.20
  114.9 5.5 %all-to-all-start.2 = ((f32[4,16,1,128,128]{3,4,1,2,0:T(8,128)}), f32[4,16,1,128,128]{3,4,1,2,0:T(8,128)}, u32[]{:S(2)}, u32[]{:S(2)}) async-start(f32[4,16,1,128,128]{3,4,1,2,0:T(8,128)} %stack.20), calls=%async_computation.2 | async-start | bytes 8388608 | tf_op jit(solution)/shard_map/all_to_all | solution.py:22
  120.4 8.1 %convolution_bitcast_fusion = f32[8192,128]{0,1:T(8,128)} fusion(f32[128,128]{1,0:T(8,128)S(1)} %fusion.147, f32[8192,128]{1,0:T(8,128)} %param.4), kind=kOutput, calls=%fused_computation.6 | convolution fusion | flops 1610612736 | bytes 8454144 | tf_op jit(solution)/shard_map/dot_general | solution.py:74
  128.5 5.6 %copy.106 = f32[8192,128]{1,0:T(8,128)} copy(f32[8192,128]{0,1:T(8,128)} %convolution_bitcast_fusion) | data formatting | bytes 8388608 | tf_op jit(solution)/shard_map/reshape | solution.py:78
  134.1 30.6 %all-to-all-done.2 = f32[4,16,1,128,128]{3,4,1,2,0:T(8,128)} async-done(((f32[4,16,1,128,128]{3,4,1,2,0:T(8,128)}), f32[4,16,1,128,128]{3,4,1,2,0:T(8,128)}, u32[]{:S(2)}, u32[]{:S(2)}) %all-to-all-start.2) | async-done | bytes 4194336 | tf_op jit(solution)/shard_map/all_to_all | solution.py:22
  164.7 2.6 copy.80
  168.1 4.8 %fusion.148 = f32[64,128,128]{2,1,0:T(8,128)S(1)} fusion(f32[64,128,128]{1,2,0:T(8,128)S(1)} %bitcast.179, f32[64,128,128]{2,1,0:T(8,128)S(1)} %bitcast.177), kind=kOutput, calls=%fused_computation.227 | convolution fusion | flops 1610612736 | bytes 12582912 | tf_op jit(solution)/shard_map/nba,nbc->nac/dot_general | solution.py:79
  173.0 4.7 %fusion.141 = (f32[8192,64]{1,0:T(8,128)}, f32[8192,64]{1,0:T(8,128)}) fusion(f32[8192,128]{1,0:T(8,128)S(1)} %bitcast.174), kind=kLoop, calls=%fused_computation.220 | loop fusion | bytes 8388608 | tf_op jit(solution)/shard_map/slice | solution.py:101
  177.7 2.8 copy.82
  181.1 44.2 %collective-permute-done = f32[8192,64]{0,1:T(8,128)} collective-permute-done((f32[8192,64]{0,1:T(8,128)S(1)}, f32[8192,64]{0,1:T(8,128)}, u32[]{:S(2)}, u32[]{:S(2)}) %collective-permute-start) | collective-permute-done | bytes 2097184 | tf_op jit(solution)/shard_map/ppermute | solution.py:35
  225.3 4.0 copy.83
  229.3 4.6 %pad_maximum_fusion = f32[8192,128]{1,0:T(8,128)S(1)} fusion(f32[8192,64]{1,0:T(8,128)} %copy.83, f32[8192,64]{1,0:T(8,128)} %get-tuple-element.8), kind=kLoop, calls=%fused_computation.7 | loop fusion | flops 1048576 | bytes 8388608 | tf_op jit(solution)/shard_map/concatenate | solution.py:101
  233.9 1.6 fusion.140
  235.5 1.5 rev.3
  237.0 2.5 pad_maximum_fusion.1
  239.5 2.0 copy-done
  241.6 1.3 gather_fusion.3
  243.7 11.7 %cholesky.137 = f32[128,128]{1,0:T(8,128)S(1)} custom-call(f32[128,128]{1,0:T(8,128)S(1)} %fusion.84), custom_call_target="Cholesky" | custom-call | tf_op jit(solution)/shard_map/jit(cholesky)/cholesky | solution.py:51
  256.8 9.8 %custom-call.27 = f32[1,128,128]{1,2,0:T(8,128)S(1)} custom-call(f32[1,128,128]{2,1,0:T(8,128)S(1)} %fusion.21), custom_call_target="InvertDiagBlocksLowerTriangular" | custom-call | tf_op jit(solution)/shard_map/jit(_cho_solve)/triangular_solve | solution.py:53
  268.0 1.7 gather_fusion.4
  270.4 11.7 %cholesky.148 = f32[128,128]{1,0:T(8,128)S(1)} custom-call(f32[128,128]{1,0:T(8,128)S(1)} %fusion.79), custom_call_target="Cholesky" | custom-call | tf_op jit(solution)/shard_map/jit(cholesky)/cholesky | solution.py:51
  283.4 9.8 %custom-call.28 = f32[1,128,128]{1,2,0:T(8,128)S(1)} custom-call(f32[1,128,128]{2,1,0:T(8,128)S(1)} %fusion.22), custom_call_target="InvertDiagBlocksLowerTriangular" | custom-call | tf_op jit(solution)/shard_map/jit(_cho_solve)/triangular_solve | solution.py:53
  294.3 1.4 gather_fusion.5
  296.7 11.7 %cholesky.159 = f32[128,128]{1,0:T(8,128)S(1)} custom-call(f32[128,128]{1,0:T(8,128)S(1)} %fusion.74), custom_call_target="Cholesky" | custom-call | tf_op jit(solution)/shard_map/jit(cholesky)/cholesky | solution.py:51
  309.8 9.8 %custom-call.29 = f32[1,128,128]{1,2,0:T(8,128)S(1)} custom-call(f32[1,128,128]{2,1,0:T(8,128)S(1)} %fusion.23), custom_call_target="InvertDiagBlocksLowerTriangular" | custom-call | tf_op jit(solution)/shard_map/jit(_cho_solve)/triangular_solve | solution.py:53
  320.4 14.7 %all_to_all.32 = f32[4,1,1,128,128]{3,4,2,1,0:T(8,128)S(1)} all-to-all(f32[4,1,1,128,128]{3,4,2,1,0:T(8,128)S(1)} %stack.21), channel_id=1, replica_groups=mesh['wide_0'=4,'wide_1'=4,'wide_2'=4,'layer'=4] {'wide_1'}, dimensions={0} | all-to-all | bytes 524288 | tf_op jit(solution)/shard_map/all_to_all | solution.py:22
  336.2 3.5 all-to-all-start.4
  339.8 4.2 fusion.4
  343.9 6.7 %all-to-all-done.4 = f32[4,4,1,128,128]{3,4,1,2,0:T(8,128)S(1)} async-done(((f32[4,4,1,128,128]{3,4,1,2,0:T(8,128)}), f32[4,4,1,128,128]{3,4,1,2,0:T(8,128)S(1)}, u32[]{:S(2)}, u32[]{:S(2)}) %all-to-all-start.4) | async-done | bytes 1048608 | tf_op jit(solution)/shard_map/all_to_all | solution.py:22
  350.6 2.6 stack.23
  353.2 6.3 %all-to-all-start.5 = ((f32[4,16,1,128,128]{3,4,1,2,0:T(8,128)}), f32[4,16,1,128,128]{3,4,1,2,0:T(8,128)}, u32[]{:S(2)}, u32[]{:S(2)}) async-start(f32[4,16,1,128,128]{3,4,1,2,0:T(8,128)} %stack.23), calls=%async_computation.5 | async-start | bytes 8388608 | tf_op jit(solution)/shard_map/all_to_all | solution.py:22
  359.5 2.5 fusion.139
  362.7 41.9 %collective-permute-done.1 = f32[8192,64]{0,1:T(8,128)S(1)} collective-permute-done((f32[8192,64]{0,1:T(8,128)S(1)}, f32[8192,64]{0,1:T(8,128)S(1)}, u32[]{:S(2)}, u32[]{:S(2)}) %collective-permute-start.1) | collective-permute-done | bytes 2097184 | tf_op jit(solution)/shard_map/ppermute | solution.py:35
  404.6 8.6 %fusion = f32[8192,128]{1,0:T(8,128)} fusion(f32[128,128]{1,0:T(8,128)S(1)} %fusion.154, f32[8192,64]{0,1:T(8,128)S(1)} %collective-permute-done.1, f32[8192,64]{0,1:T(8,128)S(1)} %get-tuple-element.4), kind=kOutput, calls=%fused_computation.9 | convolution fusion | flops 1611661312 | bytes 8454144 | tf_op jit(solution)/shard_map/dot_general | solution.py:83
  413.1 4.9 %fusion.68 = f32[64,128,128]{2,1,0:T(8,128)} fusion(f32[64,128,128]{2,1,0:T(8,128)S(1)} %bitcast.176, f32[128,128]{1,0:T(8,128)S(1)} %fusion.154), kind=kOutput, calls=%fused_computation.127 | convolution fusion | flops 1610612736 | bytes 8454144 | tf_op jit(solution)/shard_map/dot_general | solution.py:74
  418.0 2.6 copy.99
  421.5 5.7 %fusion.155 = f32[64,128,128]{2,1,0:T(8,128)} fusion(f32[64,128,128]{1,2,0:T(8,128)S(1)} %bitcast.180, f32[64,128,128]{2,1,0:T(8,128)S(1)} %copy-done.2), kind=kOutput, calls=%fused_computation.234 | convolution fusion | flops 1610612736 | bytes 12582912 | tf_op jit(solution)/shard_map/nba,nbc->nac/dot_general | solution.py:79
  (102 shorter events, 24.3 us)
Async XLA Ops:
  114.9 49.8 %all-to-all-start.2 = ((f32[4,16,1,128,128]{3,4,1,2,0:T(8,128)}), f32[4,16,1,128,128]{3,4,1,2,0:T(8,128)}, u32[]{:S(2)}, u32[]{:S(2)}) async-start(f32[4,16,1,128,128]{3,4,1,2,0:T(8,128)} %stack.20), calls=%async_computation.2 | async-start | bytes 8388608 | tf_op jit(solution)/shard_map/all_to_all | solution.py:22
  164.7 3.4 copy-start.3
  180.5 44.8 %collective-permute-start = (f32[8192,64]{0,1:T(8,128)S(1)}, f32[8192,64]{0,1:T(8,128)}, u32[]{:S(2)}, u32[]{:S(2)}) collective-permute-start(f32[8192,64]{0,1:T(8,128)S(1)} %copy.82), channel_id=1, source_target_pairs={{0,128},{4,132},{8,136},{12,140},{16,144},{20,148},{24,152},{28,15... | collective-permute-start | bytes 6291464 | tf_op jit(solution)/shard_map/ppermute | solution.py:35
  239.5 2.0 copy-start
  336.2 14.4 %all-to-all-start.4 = ((f32[4,4,1,128,128]{3,4,1,2,0:T(8,128)}), f32[4,4,1,128,128]{3,4,1,2,0:T(8,128)S(1)}, u32[]{:S(2)}, u32[]{:S(2)}) async-start(f32[4,4,1,128,128]{3,4,1,2,0:T(8,128)} %stack.22), calls=%async_computation.4 | async-start | bytes 2097152 | tf_op jit(solution)/shard_map/all_to_all | solution.py:22
  353.2 64.8 %all-to-all-start.5 = ((f32[4,16,1,128,128]{3,4,1,2,0:T(8,128)}), f32[4,16,1,128,128]{3,4,1,2,0:T(8,128)}, u32[]{:S(2)}, u32[]{:S(2)}) async-start(f32[4,16,1,128,128]{3,4,1,2,0:T(8,128)} %stack.23), calls=%async_computation.5 | async-start | bytes 8388608 | tf_op jit(solution)/shard_map/all_to_all | solution.py:22
  362.0 42.5 %collective-permute-start.1 = (f32[8192,64]{0,1:T(8,128)S(1)}, f32[8192,64]{0,1:T(8,128)S(1)}, u32[]{:S(2)}, u32[]{:S(2)}) collective-permute-start(f32[8192,64]{0,1:T(8,128)S(1)} %get-tuple-element.5), channel_id=1, source_target_pairs={{0,128},{4,132},{8,136},{12,140},{16,144},{20,148},{24,152},{28,15... | collective-permute-start | bytes 6291464 | tf_op jit(solution)/shard_map/ppermute | solution.py:35
  404.6 8.6 %copy-start.1 = (f32[2,32,2,64,128]{4,3,2,1,0:T(8,128)S(1)}, f32[2,32,2,64,128]{4,3,2,1,0:T(8,128)}, u32[]{:S(2)}) copy-start(f32[2,32,2,64,128]{4,3,2,1,0:T(8,128)} %copy-done) | copy-start | bytes 12582916
  418.0 3.5 copy-start.2
